TPU v7x, 32 devices: a whole 2x2x4 slice. The times are simulated.
32 devices in a mesh: wide: 8 (over z, core), narrow: 4 (over y, x).
Axes of the slice: x: 2, y: 2, z: 4, core: 2. Of those that a mesh axis runs over, the one named last changes fastest.
Arguments:
- points: float32 [8192, 128], P(('wide', 'narrow')), may hold values from -6 to 6
- targets: float32 [16, 8192], P(None, ('wide', 'narrow')), may hold values from -6 to 6
- start: float32 [16, 8192], P(None, ('wide', 'narrow')), may hold values from -6 to 6
- interp: float32 [8192, 128], P(('wide', 'narrow')), may hold values from -0.375 to 0.375
- skel_points: float32 [1024, 128], P('wide'), may hold values from -6 to 6
- near_leaves: int32 [64, 8], P(('wide', 'narrow')), may hold values from 0 to 7, as said below
- near_count: int32 [64], P(('wide', 'narrow')), may hold values from 1 to 8
Outputs:
- weights: float32 [16, 8192], P(None, ('wide', 'narrow'))
- residual: float32 [16, 8192], P(None, ('wide', 'narrow'))
Inputs may be any that keep to these rules, and one draw needn't show every extreme that they name: `near_leaves`: each row names 8 different leaves of the row's own subtree.
All inputs are finite; a program needn't handle non-finite values.
Results may differ from a plain program's by a relative error of at most 0.0003.
Values sent between devices are 32-bit elements; how exact they have to be, the bound alone decides.
No kernel may reach another device: no remote copies, remote signals or barrier semaphores. Data moves between devices by JAX's collectives and lax.ppermute only.
A program may use at most 64 MiB of HBM per device.

v0:
```python
import math
import jax
import jax.numpy as jnp
from jax import lax
from jax.sharding import PartitionSpec as P

ITERS = 2
ridge_shift = 1.0
step_size = 0.05
kernel_rate = 2.0
highest = lax.Precision.HIGHEST


def kernel(left_points, right_points, features):
    cross_prod = jnp.dot(
        left_points, right_points.T, precision=highest, preferred_element_type=jnp.float32
    )
    left_sq = jnp.sum(left_points * left_points, axis=1)
    right_sq = jnp.sum(right_points * right_points, axis=1)
    return jnp.exp(
        -(kernel_rate / features) * (left_sq[:, None] + right_sq[None, :] - 2.0 * cross_prod)
    )


def far_block(row_blocks, skeleton, columns, features):

    def row_group(block_points):
        kernel_vals = kernel(block_points, skeleton, features)
        return jnp.einsum("rs,ps->rp", columns, kernel_vals, precision=highest)

    pieces_out = lax.map(row_group, row_blocks)
    return jnp.transpose(pieces_out, (1, 0, 2)).reshape(columns.shape[0], -1)


def on_device(points, targets, start, interp, skel_points, near_leaves, near_count):
    leaf_dev, near_slots = near_leaves.shape
    row_total, features = points.shape
    leaf_size = row_total // leaf_dev
    rhs_count = targets.shape[0]
    skel_rank = interp.shape[1]
    block_rows = math.gcd(row_total, 512)
    row_blocks = points.reshape(row_total // block_rows, block_rows, features)
    own_blocks = points.reshape(leaf_dev, leaf_size, features)
    subtree = lax.all_gather(points, "narrow", axis=0, tiled=True).reshape(-1, leaf_size, features)
    neighbours = subtree[near_leaves]
    cross_prod = jnp.einsum("ipd,ikqd->ikpq", own_blocks, neighbours, precision=highest)
    own_sq = jnp.sum(own_blocks * own_blocks, axis=-1)
    near_sq = jnp.sum(neighbours * neighbours, axis=-1)
    live_mask = (jnp.arange(near_slots, dtype=jnp.int32)[None, :] < near_count[:, None]).astype(
        jnp.float32
    )
    distance = own_sq[:, None, :, None] + near_sq[:, :, None, :] - 2.0 * cross_prod
    near_kern = jnp.exp(-(kernel_rate / features) * distance) * live_mask[:, :, None, None]
    group_index = lax.axis_index("wide")
    weights = start
    residual = targets
    for iteration in range(ITERS):
        gathered = lax.all_gather(weights, "narrow", axis=1, tiled=True).reshape(
            rhs_count, -1, leaf_size
        )
        picked = gathered[:, near_leaves]
        near_term = jnp.einsum("ikpq,rikq->rip", near_kern, picked, precision=highest).reshape(
            rhs_count, row_total
        )
        node_local = jnp.dot(weights, interp, precision=highest, preferred_element_type=jnp.float32)
        summed = lax.psum(node_local, "narrow")
        skel_table = lax.all_gather(summed, "wide", axis=1, tiled=True)
        owner_node = jnp.arange(skel_table.shape[1], dtype=jnp.int32) // skel_rank
        skel_table = jnp.where((owner_node == group_index)[None, :], jnp.float32(0.0), skel_table)
        far_term = far_block(
            row_blocks,
            lax.all_gather(skel_points, "wide", axis=0, tiled=True),
            skel_table,
            features,
        )
        residual = targets - (ridge_shift * weights + (near_term + far_term))
        weights = weights + step_size * residual
    return (weights, residual)


def solution(mesh):
    in_specs = (
        P(("wide", "narrow"), None),
        P(None, ("wide", "narrow")),
        P(None, ("wide", "narrow")),
        P(("wide", "narrow"), None),
        P("wide", None),
        P(("wide", "narrow"), None),
        P(("wide", "narrow")),
    )
    out_specs = (P(None, ("wide", "narrow")), P(None, ("wide", "narrow")))
    return jax.shard_map(
        on_device, mesh=mesh, in_specs=in_specs, out_specs=out_specs, check_vma=False
    )
```

profile of v0, /device:TPU:0, one launch (start us, length us, event | category | flops | bytes accessed | tf_op | source)
XLA Modules:
  0.0 100.6 jit_solution(13071996611529464808)
XLA Ops:
  0.6 0.7 compare_select_fusion
  1.5 11.9 %all_gather.20 = f32[1024,128]{1,0:T(8,128)S(1)} all-gather(f32[256,128]{1,0:T(8,128)} %param.7), channel_id=1, replica_groups=mesh['wide'=8,'narrow'=4] {'narrow'}, dimensions={0}, use_global_device_ids=true | all-gather | bytes 655360 | tf_op jit(solution)/shard_map/all_gather | solution.py:44
  13.3 0.6 gather_fusion.1
  14.0 0.3 multiply_reduce_fusion
  14.3 0.5 copy-done.1
  15.0 0.6 copy-done.5
  15.7 1.2 %fusion.7 = f32[2,8,128,128]{2,3,1,0:T(8,128)S(1)} fusion(f32[2,8,128,128]{3,2,1,0:T(8,128)S(1)} %bitcast.65, f32[2,128,128,1]{2,1,3,0:T(8,128)S(1)} %bitcast.67, f32[2,8]{1,0:T(2,128)S(1)} %compare_convert_fusion, f32[2,8,128]{2,1,0:T(8,128)S(1)} %multiply_reduce_fusion, f32[2,128]{1,0:T(2,128)S(1)} %bitcast.70), kind=kOutput, calls=%fused_computation.12 | convolution fusion | flops 403963904 | bytes 2237504 | tf_op jit(solution)/shard_map/ipd,ikqd->ikpq/dot_general | solution.py:46
  16.9 7.9 %all_gather.19 = f32[16,1024]{1,0:T(8,128)S(1)} all-gather(f32[16,256]{1,0:T(8,128)S(1)} %copy-done.2), channel_id=1, replica_groups=mesh['wide'=8,'narrow'=4] {'narrow'}, dimensions={1}, use_global_device_ids=true | all-gather | bytes 81920 | tf_op jit(solution)/shard_map/all_gather | solution.py:58
  24.8 0.6 gather_fusion
  25.4 0.6 convolution_bitcast_fusion.1
  26.0 0.2 copy-done.4
  26.2 15.2 %all_gather.22 = f32[1024,128]{1,0:T(8,128)S(1)} all-gather(f32[128,128]{1,0:T(8,128)S(1)} %copy-done.4), channel_id=1, replica_groups=mesh['wide'=8,'narrow'=4] {'wide'}, dimensions={0}, use_global_device_ids=true | all-gather | bytes 589824 | tf_op jit(solution)/shard_map/all_gather | solution.py:72
  41.4 0.2 multiply_reduce_fusion.1
  41.6 1.2 %fusion.2 = f32[256,1024]{1,0:T(8,128)S(1)} fusion(f32[256,128]{1,0:T(8,128)S(1)} %copy-done.1, f32[1024,128]{1,0:T(8,128)S(1)} %all_gather.22, f32[1024]{0:T(1024)S(1)} %multiply_reduce_fusion.1, f32[256]{0:T(256)S(1)} %multiply_reduce_fusion.2), kind=kOutput, calls=%fused_computation.6 | convolution fusion | flops 403701760 | bytes 1709056 | tf_op jit(solution)/shard_map/while/body/eval_jaxpr/dot_general | solution.py:15
  43.0 9.1 %psum.14 = f32[16,128]{1,0:T(8,128)S(1)} all-reduce(f32[16,128]{1,0:T(8,128)S(1)} %fusion.26), channel_id=1, replica_groups=mesh['wide'=8,'narrow'=4] {'narrow'}, use_global_device_ids=true, to_apply=%region_2.0 | all-reduce | flops 2048 | bytes 16384 | tf_op jit(solution)/shard_map/psum | solution.py:66
  52.1 14.0 %all_gather.21 = f32[16,1024]{1,0:T(8,128)S(1)} all-gather(f32[16,128]{1,0:T(8,128)S(1)} %psum.14), channel_id=1, replica_groups=mesh['wide'=8,'narrow'=4] {'wide'}, dimensions={1}, use_global_device_ids=true | all-gather | bytes 73728 | tf_op jit(solution)/shard_map/all_gather | solution.py:67
  66.1 0.9 fusion.13
  67.0 7.6 %all_gather.23 = f32[16,1024]{1,0:T(8,128)S(1)} all-gather(f32[16,256]{1,0:T(8,128)S(1)} %fusion.13), channel_id=1, replica_groups=mesh['wide'=8,'narrow'=4] {'narrow'}, dimensions={1}, use_global_device_ids=true | all-gather | bytes 81920 | tf_op jit(solution)/shard_map/all_gather | solution.py:58
  74.6 0.6 gather_fusion.2
  75.2 0.6 convolution_bitcast_fusion
  75.8 0.2 fusion.27
  76.0 9.1 %psum.15 = f32[16,128]{1,0:T(8,128)S(1)} all-reduce(f32[16,128]{1,0:T(8,128)S(1)} %fusion.27), channel_id=1, replica_groups=mesh['wide'=8,'narrow'=4] {'narrow'}, use_global_device_ids=true, to_apply=%region_4.5 | all-reduce | flops 2048 | bytes 16384 | tf_op jit(solution)/shard_map/psum | solution.py:66
  85.1 14.0 %all_gather.24 = f32[16,1024]{1,0:T(8,128)S(1)} all-gather(f32[16,128]{1,0:T(8,128)S(1)} %psum.15), channel_id=1, replica_groups=mesh['wide'=8,'narrow'=4] {'wide'}, dimensions={1}, use_global_device_ids=true | all-gather | bytes 73728 | tf_op jit(solution)/shard_map/all_gather | solution.py:67
  99.0 1.5 %multiply_add_fusion = (f32[16,256]{1,0:T(8,128)}, f32[16,256]{1,0:T(8,128)}) fusion(f32[16,256]{1,0:T(8,128)S(1)} %fusion.13, f32[16,256]{1,0:T(8,128)S(1)} %copy-done.3, f32[256,1024]{1,0:T(8,128)S(1)} %fusion.2, f32[16,1024]{1,0:T(8,128)S(1)} %all_gather.24, pred[1024]{0:T(1024)(128)(4,1)S(1)} %fusion.20, f32[2,2,8,128]{3,2,1,0:T(8,128)S(1)} %convolution_bitcast_fusion), kind=kOutput, calls=%fused_computation.34 | convolution fusion | flops 50368512 | bytes 1197056 | tf_op jit(solution)/shard_map/while/body/eval_jaxpr/rs,ps->rp/dot_general | solution.py:29
  (17 shorter events, 0.5 us)
Async XLA Ops:
  0.6 42.2 %copy-start = (f32[256,128]{1,0:T(8,128)S(1)}, f32[256,128]{1,0:T(8,128)}, u32[]{:S(2)}) copy-start(f32[256,128]{1,0:T(8,128)} %param.10) | copy-start | bytes 393220
  13.9 0.9 copy-start.1
  15.0 0.7 copy-start.5
  15.7 1.2 %copy-start.2 = (f32[16,256]{1,0:T(8,128)S(1)}, f32[16,256]{1,0:T(8,128)}, u32[]{:S(2)}) copy-start(f32[16,256]{1,0:T(8,128)} %param.9) | copy-start | bytes 49156
  25.4 0.8 copy-start.4
  52.1 14.0 %copy-start.3 = (f32[16,256]{1,0:T(8,128)S(1)}, f32[16,256]{1,0:T(8,128)}, u32[]{:S(2)}) copy-start(f32[16,256]{1,0:T(8,128)} %param.8) | copy-start | bytes 49156
where the time goes:
time: 101 us
  blocking collectives  88.6 us (88%)
  matrix products  6.43 us (6%)
  local copies, waits for them, and re-layouts  3.27 us (3%)
  other arithmetic  1.46 us (1%)
    all_gather x2, blocking collectives, on_device(): skel_table = lax.all_gather(summed, 'wide', axis=1, tiled=True)  27.9 us
    psum x2, blocking collectives, on_device(): summed = lax.psum(node_local, 'narrow')  18.2 us
    all_gather x2, blocking collectives, on_device(): lax.all_gather(weights, 'narrow', axis=1, tiled=True)  15.5 us
    all_gather x1, blocking collectives, on_device(): lax.all_gather(skel_points, 'wide', axis=0, tiled=True)  15.2 us
    all_gather x1, blocking collectives, on_device(): lax.all_gather(points, 'narrow', axis=0, tiled=True)  11.9 us
    dot_general x2, matrix products, row_group(): return jnp.einsum('rs,ps->rp', columns, kernel_vals, precision=highest)  2.48 us

commit v1 on v0

--- a/solution.py
+++ b/solution.py
@@ -55,7 +55,7 @@
     weights = start
     residual = targets
     for iteration in range(ITERS):
-        gathered = lax.all_gather(weights, "narrow", axis=1, tiled=True).reshape(
+        gathered = jnp.concatenate(lax.all_gather(weights, "narrow"), axis=1).reshape(
             rhs_count, -1, leaf_size
         )
         picked = gathered[:, near_leaves]

time: 101 us -> 101 us (level)
  no operation moved by 1% of the time
where the time goes in v1:
time: 101 us
  blocking collectives  88.6 us (88%)
  matrix products  6.42 us (6%)
  local copies, waits for them, and re-layouts  3.43 us (3%)
  other arithmetic  1.46 us (1%)
    all_gather x2, blocking collectives, on_device(): skel_table = lax.all_gather(summed, 'wide', axis=1, tiled=True)  27.9 us
    psum x2, blocking collectives, on_device(): summed = lax.psum(node_local, 'narrow')  18.2 us
    all_gather x2, blocking collectives, on_device(): lax.all_gather(weights, 'narrow')  15.5 us
    all_gather x1, blocking collectives, on_device(): lax.all_gather(skel_points, 'wide', axis=0, tiled=True)  15.2 us
    all_gather x1, blocking collectives, on_device(): lax.all_gather(points, 'narrow', axis=0, tiled=True)  11.9 us
    dot_general x2, matrix products, row_group(): return jnp.einsum('rs,ps->rp', columns, kernel_vals, precision=highest)  2.48 us

profile of v1, /device:TPU:0, one launch (start us, length us, event | category | flops | bytes accessed | tf_op | source)
XLA Modules:
  0.0 100.8 jit_solution(14994179904077761409)
XLA Ops:
  0.6 0.7 compare_select_fusion
  1.5 11.9 %all_gather.27 = f32[1024,128]{1,0:T(8,128)S(1)} all-gather(f32[256,128]{1,0:T(8,128)} %param.7), channel_id=1, replica_groups=mesh['wide'=8,'narrow'=4] {'narrow'}, dimensions={0}, use_global_device_ids=true | all-gather | bytes 655360 | tf_op jit(solution)/shard_map/all_gather | solution.py:44
  13.3 0.6 gather_fusion.1
  14.0 0.3 multiply_reduce_fusion
  14.3 0.5 copy-done.1
  15.0 0.6 copy-done.5
  15.7 1.2 %fusion.7 = f32[2,8,128,128]{2,3,1,0:T(8,128)S(1)} fusion(f32[2,8,128,128]{3,2,1,0:T(8,128)S(1)} %bitcast.63, f32[2,128,128,1]{2,1,3,0:T(8,128)S(1)} %bitcast.65, f32[2,8]{1,0:T(2,128)S(1)} %compare_convert_fusion, f32[2,8,128]{2,1,0:T(8,128)S(1)} %multiply_reduce_fusion, f32[2,128]{1,0:T(2,128)S(1)} %bitcast.72), kind=kOutput, calls=%fused_computation.12 | convolution fusion | flops 403963904 | bytes 2237504 | tf_op jit(solution)/shard_map/ipd,ikqd->ikpq/dot_general | solution.py:46
  16.9 7.9 %all-gather = f32[64,256]{1,0:T(8,128)S(1)} all-gather(f32[16,256]{1,0:T(8,128)S(1)} %copy-done.2), channel_id=2, replica_groups=mesh['wide'=8,'narrow'=4] {'narrow'}, dimensions={0}, use_global_device_ids=true | all-gather | bytes 81920 | tf_op jit(solution)/shard_map/all_gather | solution.py:58
  24.9 0.6 gather_fusion
  25.5 0.6 convolution_bitcast_fusion.1
  26.1 0.2 copy-done.4
  26.3 15.2 %all_gather.29 = f32[1024,128]{1,0:T(8,128)S(1)} all-gather(f32[128,128]{1,0:T(8,128)S(1)} %copy-done.4), channel_id=1, replica_groups=mesh['wide'=8,'narrow'=4] {'wide'}, dimensions={0}, use_global_device_ids=true | all-gather | bytes 589824 | tf_op jit(solution)/shard_map/all_gather | solution.py:72
  41.5 0.2 multiply_reduce_fusion.1
  41.7 1.1 %fusion.2 = f32[256,1024]{1,0:T(8,128)S(1)} fusion(f32[256,128]{1,0:T(8,128)S(1)} %copy-done.1, f32[1024,128]{1,0:T(8,128)S(1)} %all_gather.29, f32[1024]{0:T(1024)S(1)} %multiply_reduce_fusion.1, f32[256]{0:T(256)S(1)} %multiply_reduce_fusion.2), kind=kOutput, calls=%fused_computation.6 | convolution fusion | flops 403701760 | bytes 1709056 | tf_op jit(solution)/shard_map/while/body/eval_jaxpr/dot_general | solution.py:15
  43.1 9.1 %psum.14 = f32[16,128]{1,0:T(8,128)S(1)} all-reduce(f32[16,128]{1,0:T(8,128)S(1)} %fusion.26), channel_id=1, replica_groups=mesh['wide'=8,'narrow'=4] {'narrow'}, use_global_device_ids=true, to_apply=%region_2.0 | all-reduce | flops 2048 | bytes 16384 | tf_op jit(solution)/shard_map/psum | solution.py:66
  52.2 14.0 %all_gather.28 = f32[16,1024]{1,0:T(8,128)S(1)} all-gather(f32[16,128]{1,0:T(8,128)S(1)} %psum.14), channel_id=1, replica_groups=mesh['wide'=8,'narrow'=4] {'wide'}, dimensions={1}, use_global_device_ids=true | all-gather | bytes 73728 | tf_op jit(solution)/shard_map/all_gather | solution.py:67
  66.1 0.9 fusion.13
  67.1 7.6 %all-gather.1 = f32[64,256]{1,0:T(8,128)S(1)} all-gather(f32[16,256]{1,0:T(8,128)S(1)} %fusion.13), channel_id=3, replica_groups=mesh['wide'=8,'narrow'=4] {'narrow'}, dimensions={0}, use_global_device_ids=true | all-gather | bytes 81920 | tf_op jit(solution)/shard_map/all_gather | solution.py:58
  74.8 0.6 gather_fusion.2
  75.4 0.6 convolution_bitcast_fusion
  76.0 0.2 fusion.27
  76.2 9.1 %psum.15 = f32[16,128]{1,0:T(8,128)S(1)} all-reduce(f32[16,128]{1,0:T(8,128)S(1)} %fusion.27), channel_id=1, replica_groups=mesh['wide'=8,'narrow'=4] {'narrow'}, use_global_device_ids=true, to_apply=%region_4.5 | all-reduce | flops 2048 | bytes 16384 | tf_op jit(solution)/shard_map/psum | solution.py:66
  85.3 14.0 %all_gather.32 = f32[16,1024]{1,0:T(8,128)S(1)} all-gather(f32[16,128]{1,0:T(8,128)S(1)} %psum.15), channel_id=1, replica_groups=mesh['wide'=8,'narrow'=4] {'wide'}, dimensions={1}, use_global_device_ids=true | all-gather | bytes 73728 | tf_op jit(solution)/shard_map/all_gather | solution.py:67
  99.2 1.5 %multiply_add_fusion = (f32[16,256]{1,0:T(8,128)}, f32[16,256]{1,0:T(8,128)}) fusion(f32[16,256]{1,0:T(8,128)S(1)} %fusion.13, f32[16,256]{1,0:T(8,128)S(1)} %copy-done.3, f32[256,1024]{1,0:T(8,128)S(1)} %fusion.2, f32[16,1024]{1,0:T(8,128)S(1)} %all_gather.32, pred[1024]{0:T(1024)(128)(4,1)S(1)} %fusion.20, f32[2,2,8,128]{3,2,1,0:T(8,128)S(1)} %convolution_bitcast_fusion), kind=kOutput, calls=%fused_computation.34 | convolution fusion | flops 50368512 | bytes 1197056 | tf_op jit(solution)/shard_map/while/body/eval_jaxpr/rs,ps->rp/dot_general | solution.py:29
  (21 shorter events, 0.7 us)
Async XLA Ops:
  0.6 42.3 %copy-start = (f32[256,128]{1,0:T(8,128)S(1)}, f32[256,128]{1,0:T(8,128)}, u32[]{:S(2)}) copy-start(f32[256,128]{1,0:T(8,128)} %param.10) | copy-start | bytes 393220
  13.9 0.9 copy-start.1
  15.0 0.7 copy-start.5
  15.7 1.2 %copy-start.2 = (f32[16,256]{1,0:T(8,128)S(1)}, f32[16,256]{1,0:T(8,128)}, u32[]{:S(2)}) copy-start(f32[16,256]{1,0:T(8,128)} %param.9) | copy-start | bytes 49156
  25.5 0.8 copy-start.4
  52.2 14.0 %copy-start.3 = (f32[16,256]{1,0:T(8,128)S(1)}, f32[16,256]{1,0:T(8,128)}, u32[]{:S(2)}) copy-start(f32[16,256]{1,0:T(8,128)} %param.8) | copy-start | bytes 49156
